TPU v7x, 32 devices: a whole 2x2x4 slice. The times are simulated.
32 devices in a mesh: rep: 4 (over x, core), fsdp: 8 (over z, y).
Axes of the slice: x: 2, y: 2, z: 4, core: 2. Of those that a mesh axis runs over, the one named last changes fastest.
Arguments:
- features: bfloat16 [4096, 1280], P(('rep', 'fsdp')), may hold values from -6 to 6
- cotangent: bfloat16 [4096, 1280], P(('rep', 'fsdp')), may hold values from -1 to 1
- clip_lengths: int32 [4, 8], P('rep'), may hold values from 96 to 128, as said below
- group_clips: int32 [4], P('rep'), may hold values from 6 to 8, as said below
- outer_attention: float32 [2, 1280, 5120], P(None, 'fsdp')
- outer_feedforward: float32 [2, 1280, 10240], P(None, 'fsdp')
- outer_vectors: float32 [2, 12, 1280], P(None, None, 'fsdp')
- moments_attention: float32 [4, 2, 1280, 5120], P('rep', None, 'fsdp')
- moments_feedforward: float32 [4, 2, 1280, 10240], P('rep', None, 'fsdp')
- moments_vectors: float32 [4, 2, 12, 1280], P('rep', None, None, 'fsdp')
Outputs:
- block_output: bfloat16 [4096, 1280], P(('rep', 'fsdp'))
- input_grad: float32 [4096, 1280], P(('rep', 'fsdp'))
- group_attention: float32 [4, 3, 1280, 5120], P('rep', None, 'fsdp')
- group_feedforward: float32 [4, 3, 1280, 10240], P('rep', None, 'fsdp')
- group_vectors: float32 [4, 3, 12, 1280], P('rep', None, None, 'fsdp')
- group_weights: float32 [4, 1280, 15372], P('rep', 'fsdp')
- next_attention: float32 [3, 1280, 5120], P(None, 'fsdp')
- next_feedforward: float32 [3, 1280, 10240], P(None, 'fsdp')
- next_vectors: float32 [3, 12, 1280], P(None, None, 'fsdp')
- copy_attention: bfloat16 [1280, 5120], P('fsdp')
- copy_feedforward: bfloat16 [1280, 10240], P('fsdp')
- copy_vectors: bfloat16 [12, 1280], P(None, 'fsdp')
Inputs may be any that keep to these rules, and one draw needn't show every extreme that they name: `clip_lengths`: some clip has exactly 128 valid tokens and some exactly 96. Group g holds clips in its slots 0 to group_clips[g] - 1 and none in the others; some group has all 8 and some 8 - 2.
All inputs are finite; a program needn't handle non-finite values.
Results may differ from a plain program's by a relative error of at most 0.012.
The roundings to bfloat16 on the way count: a program that leaves them out, or rounds other values in their place, can miss the bound.
Values may be sent and summed in bfloat16 or wider, within the bound.
A program may use at most 448 MiB of HBM per device.

v0:
```python
from functools import partial
import jax
import jax.numpy as jnp
from jax import lax
from jax.sharding import PartitionSpec as P

D = 1280
HEADS = 16
HD = 80
FF = 5120
STEP = 3
NORM_EPS = 1e-05
MASKED = -1e30
ADAM_RATE = 0.03
ADAM_DECAY = 0.1
ADAM_BETA = 0.5
ADAM_EPS = 1e-08
OUTER_RATE = 0.7
OUTER_MOMENTUM = 0.5


def contract_last(left, right):
    return lax.dot_general(
        left, right, (((1,), (1,)), ((), ())), preferred_element_type=jnp.float32
    )


def contract_rows(left, right):
    return lax.dot_general(
        left, right, (((0,), (0,)), ((), ())), preferred_element_type=jnp.float32
    )


def normalize(inputs, gain_row, shift_row):
    average = jnp.mean(inputs, axis=-1, keepdims=True)
    centered = inputs - average
    reciprocal = lax.rsqrt(jnp.mean(centered * centered, axis=-1, keepdims=True) + NORM_EPS)
    unit_rows = centered * reciprocal
    return (unit_rows * gain_row + shift_row, unit_rows, reciprocal)


def normalize_back(incoming, unit_rows, reciprocal, gain_row):
    scaled = incoming * gain_row
    centered = scaled - jnp.mean(scaled, axis=-1, keepdims=True)
    return reciprocal * (
        centered - unit_rows * jnp.mean(scaled * unit_rows, axis=-1, keepdims=True)
    )


def adamw_step(weight, gradient, moments, decay_rate):
    first_moment = ADAM_BETA * moments[0] + (1.0 - ADAM_BETA) * gradient
    second_moment = ADAM_BETA * moments[1] + (1.0 - ADAM_BETA) * gradient * gradient
    correction = 1.0 - ADAM_BETA**STEP
    direction = first_moment / correction / (jnp.sqrt(second_moment / correction) + ADAM_EPS)
    return (weight - ADAM_RATE * (direction + decay_rate * weight), first_moment, second_moment)


def outer_step(master, mean_delta, momentum_old):
    momentum = OUTER_MOMENTUM * momentum_old - mean_delta
    outer_next = master - OUTER_RATE * (OUTER_MOMENTUM * momentum - mean_delta)
    return jnp.stack([mean_delta, momentum, outer_next])


def shards(
    features,
    cotangent,
    clip_lengths,
    group_clips,
    outer_attention,
    outer_feedforward,
    outer_vectors,
    moments_attention,
    moments_feedforward,
    moments_vectors,
):
    tokens_here = features.shape[0]
    scale = HD ** (-0.5)
    clip_slot = lax.axis_index("fsdp")
    clip_length = lax.dynamic_index_in_dim(clip_lengths[0], clip_slot, keepdims=False)
    live_clip = clip_slot < group_clips[0]
    positions = jnp.arange(tokens_here, dtype=jnp.int32)
    key_valid = positions < clip_length
    row_valid = key_valid & live_clip
    masters = (outer_attention[0], outer_feedforward[0], outer_vectors[0])
    copies = (
        masters[0].astype(jnp.bfloat16),
        masters[1].astype(jnp.bfloat16),
        masters[2].astype(jnp.bfloat16),
    )
    full_attention, full_feedforward, full_vectors = (
        lax.all_gather(copies[0], "fsdp", axis=0, tiled=True),
        lax.all_gather(copies[1], "fsdp", axis=0, tiled=True),
        lax.all_gather(copies[2], "fsdp", axis=1, tiled=True),
    )
    vectors = full_vectors.astype(jnp.float32)
    inputs = features.astype(jnp.float32)
    normed_one, unit_one, scale_one = normalize(inputs, vectors[0], vectors[1])
    layer_one = normed_one.astype(jnp.bfloat16)
    qkv_bias = jnp.concatenate([vectors[2], jnp.zeros_like(vectors[2]), vectors[3]])
    projected = (
        jnp.dot(layer_one, full_attention[:, : 3 * D], preferred_element_type=jnp.float32)
        + qkv_bias
    ).astype(jnp.bfloat16)
    query_heads = projected[:, :D].reshape(tokens_here, HEADS, HD)
    key_heads = projected[:, D : 2 * D].reshape(tokens_here, HEADS, HD)
    value_heads = projected[:, 2 * D :].reshape(tokens_here, HEADS, HD)

    def score_block():
        raw_scores = (
            jnp.einsum("qhd,khd->hqk", query_heads, key_heads, preferred_element_type=jnp.float32)
            * scale
        )
        return jnp.where(key_valid[None, None, :], raw_scores, MASKED)

    scores = score_block()
    top_score = jnp.max(scores, axis=-1, keepdims=True)
    exponent = jnp.exp(scores - top_score)
    totals = jnp.sum(exponent, axis=-1, keepdims=True)
    attention_probs = exponent / totals
    log_totals = top_score + jnp.log(totals)
    attended = jnp.einsum(
        "hqk,khd->qhd",
        attention_probs.astype(jnp.bfloat16),
        value_heads,
        preferred_element_type=jnp.float32,
    )
    attended = attended.reshape(tokens_here, D).astype(jnp.bfloat16)
    attention_branch = contract_last(attended, full_attention[:, 3 * D :]) + vectors[4]
    middle = inputs + attention_branch
    normed_two, unit_two, scale_two = normalize(middle, vectors[5], vectors[6])
    layer_two = normed_two.astype(jnp.bfloat16)
    pre_activation = jnp.dot(
        layer_two, full_feedforward[:, :FF], preferred_element_type=jnp.float32
    ) + vectors[8:].reshape(FF)
    activation, gelu_backward = jax.vjp(partial(jax.nn.gelu, approximate=False), pre_activation)
    activation_low = activation.astype(jnp.bfloat16)
    feedforward_branch = contract_last(activation_low, full_feedforward[:, FF:]) + vectors[7]
    block_output = (middle + feedforward_branch).astype(jnp.bfloat16)
    back_attention, back_feedforward, back_vectors = (
        lax.all_gather(copies[0], "fsdp", axis=0, tiled=True),
        lax.all_gather(copies[1], "fsdp", axis=0, tiled=True),
        lax.all_gather(copies[2], "fsdp", axis=1, tiled=True),
    )
    gain_rows = back_vectors.astype(jnp.float32)
    upstream = cotangent.astype(jnp.float32) * row_valid[:, None].astype(jnp.float32)
    upstream_low = upstream.astype(jnp.bfloat16)
    grad_down_bias = jnp.sum(upstream_low, axis=0, dtype=jnp.float32)
    grad_activation = jnp.dot(
        upstream_low, back_feedforward[:, FF:], preferred_element_type=jnp.float32
    )
    grad_pre = gelu_backward(grad_activation)[0].astype(jnp.bfloat16)
    grad_up_bias = jnp.sum(grad_pre, axis=0, dtype=jnp.float32)
    grad_two = contract_last(grad_pre, back_feedforward[:, :FF])
    grad_gain_two = jnp.sum(grad_two * unit_two, axis=0)
    grad_shift_two = jnp.sum(grad_two, axis=0)
    grad_middle = upstream + normalize_back(grad_two, unit_two, scale_two, gain_rows[5])
    middle_low = grad_middle.astype(jnp.bfloat16)
    grad_out_bias = jnp.sum(middle_low, axis=0, dtype=jnp.float32)
    grad_attended = jnp.dot(
        middle_low, back_attention[:, 3 * D :], preferred_element_type=jnp.float32
    ).astype(jnp.bfloat16)
    grad_heads = grad_attended.reshape(tokens_here, HEADS, HD)
    attention_probs = jnp.exp(score_block() - log_totals)
    grad_probs = jnp.einsum(
        "qhd,khd->hqk", grad_heads, value_heads, preferred_element_type=jnp.float32
    )
    row_dot = jnp.sum(attention_probs * grad_probs, axis=-1, keepdims=True)
    grad_scores = (attention_probs * (grad_probs - row_dot)).astype(jnp.bfloat16)
    grad_queries = (
        jnp.einsum("hqk,khd->qhd", grad_scores, key_heads, preferred_element_type=jnp.float32)
        * scale
    ).reshape(tokens_here, D)
    grad_keys = (
        jnp.einsum("hqk,qhd->khd", grad_scores, query_heads, preferred_element_type=jnp.float32)
        * scale
    ).reshape(tokens_here, D)
    grad_values = jnp.einsum(
        "hqk,qhd->khd",
        attention_probs.astype(jnp.bfloat16),
        grad_heads,
        preferred_element_type=jnp.float32,
    ).reshape(tokens_here, D)
    grad_qkv = jnp.concatenate([grad_queries, grad_keys, grad_values], axis=1).astype(jnp.bfloat16)
    grad_query_bias = jnp.sum(grad_qkv[:, :D], axis=0, dtype=jnp.float32)
    grad_value_bias = jnp.sum(grad_qkv[:, 2 * D :], axis=0, dtype=jnp.float32)
    grad_one = contract_last(grad_qkv, back_attention[:, : 3 * D])
    grad_gain_one = jnp.sum(grad_one * unit_one, axis=0)
    grad_shift_one = jnp.sum(grad_one, axis=0)
    input_grad = grad_middle + normalize_back(grad_one, unit_one, scale_one, gain_rows[0])
    vector_rows = jnp.stack(
        [
            grad_gain_one,
            grad_shift_one,
            grad_query_bias,
            grad_value_bias,
            grad_out_bias,
            grad_gain_two,
            grad_shift_two,
            grad_down_bias,
        ]
    )
    grad_vectors = jnp.concatenate([vector_rows, grad_up_bias.reshape(4, D)], axis=0)
    owned_attention = lax.psum_scatter(
        jnp.concatenate(
            [contract_rows(layer_one, grad_qkv), contract_rows(middle_low, attended)], axis=1
        ),
        "fsdp",
        scatter_dimension=0,
        tiled=True,
    )
    owned_feedforward = lax.psum_scatter(
        jnp.concatenate(
            [contract_rows(layer_two, grad_pre), contract_rows(upstream_low, activation_low)],
            axis=1,
        ),
        "fsdp",
        scatter_dimension=0,
        tiled=True,
    )
    owned_vectors = lax.psum_scatter(grad_vectors, "fsdp", scatter_dimension=1, tiled=True)
    new_attention, first_attention, second_attention = adamw_step(
        masters[0], owned_attention, moments_attention[0], ADAM_DECAY
    )
    new_feedforward, first_feedforward, second_feedforward = adamw_step(
        masters[1], owned_feedforward, moments_feedforward[0], ADAM_DECAY
    )
    new_vectors, first_vectors, second_vectors = adamw_step(
        masters[2], owned_vectors, moments_vectors[0], 0.0
    )
    summed = (
        lax.psum_scatter(
            (new_attention - masters[0]).astype(jnp.bfloat16),
            "rep",
            scatter_dimension=1,
            tiled=True,
        ).astype(jnp.float32),
        lax.psum_scatter(
            (new_feedforward - masters[1]).astype(jnp.bfloat16),
            "rep",
            scatter_dimension=1,
            tiled=True,
        ).astype(jnp.float32),
        lax.psum_scatter(
            (new_vectors - masters[2]).astype(jnp.bfloat16), "rep", scatter_dimension=0, tiled=True
        ).astype(jnp.float32),
    )
    replicas = lax.axis_size("rep")
    replica_index = lax.axis_index("rep")
    attention_cols = 4 * D // replicas
    feedforward_cols = 2 * FF // replicas
    vector_count = 12 // replicas

    def owned_part(array, dim, count):
        return lax.dynamic_slice_in_dim(array, replica_index * count, count, dim)

    part_attention = outer_step(
        owned_part(masters[0], 1, attention_cols),
        summed[0] / replicas,
        owned_part(outer_attention[1], 1, attention_cols),
    )
    part_feedforward = outer_step(
        owned_part(masters[1], 1, feedforward_cols),
        summed[1] / replicas,
        owned_part(outer_feedforward[1], 1, feedforward_cols),
    )
    part_vectors = outer_step(
        owned_part(masters[2], 0, vector_count),
        summed[2] / replicas,
        owned_part(outer_vectors[1], 0, vector_count),
    )
    next_attention, next_feedforward, next_vectors = (
        lax.all_gather(part_attention, "rep", axis=2, tiled=True),
        lax.all_gather(part_feedforward, "rep", axis=2, tiled=True),
        lax.all_gather(part_vectors, "rep", axis=1, tiled=True),
    )
    copy_attention = next_attention[2].astype(jnp.bfloat16)
    copy_feedforward = next_feedforward[2].astype(jnp.bfloat16)
    copy_vectors = next_vectors[2].astype(jnp.bfloat16)
    group_attention = jnp.stack([owned_attention, first_attention, second_attention])[None]
    group_feedforward = jnp.stack([owned_feedforward, first_feedforward, second_feedforward])[None]
    group_vectors = jnp.stack([owned_vectors, first_vectors, second_vectors])[None]
    group_weights = jnp.concatenate([new_attention, new_feedforward, new_vectors.T], axis=1)[None]
    return (
        block_output,
        input_grad,
        group_attention,
        group_feedforward,
        group_vectors,
        group_weights,
        next_attention,
        next_feedforward,
        next_vectors,
        copy_attention,
        copy_feedforward,
        copy_vectors,
    )


def solution(mesh):
    in_specs = (
        P(("rep", "fsdp"), None),
        P(("rep", "fsdp"), None),
        P("rep", None),
        P("rep"),
        P(None, "fsdp", None),
        P(None, "fsdp", None),
        P(None, None, "fsdp"),
        P("rep", None, "fsdp", None),
        P("rep", None, "fsdp", None),
        P("rep", None, None, "fsdp"),
    )
    out_specs = (
        P(("rep", "fsdp"), None),
        P(("rep", "fsdp"), None),
        P("rep", None, "fsdp", None),
        P("rep", None, "fsdp", None),
        P("rep", None, None, "fsdp"),
        P("rep", "fsdp", None),
        P(None, "fsdp", None),
        P(None, "fsdp", None),
        P(None, None, "fsdp"),
        P("fsdp", None),
        P("fsdp", None),
        P(None, "fsdp"),
    )
    return jax.shard_map(shards, mesh=mesh, in_specs=in_specs, out_specs=out_specs, check_vma=False)
```

profile of v0, /device:TPU:0, one launch (start us, length us, event | category | flops | bytes accessed | tf_op | source)
XLA Modules:
  0.0 2351.6 jit_solution(7769149582330624274)
XLA Ops:
  7.2 3.3 bitcast_convert_fusion.1
  10.6 5.0 bitcast_convert_fusion
  17.1 33.6 %all-gather = bf16[8,160,12]{1,2,0:T(8,128)(2,1)S(1)} all-gather(bf16[1,160,12]{1,2,0:T(8,128)(2,1)S(1)} %copy.142), channel_id=1, replica_groups=mesh['rep'=4,'fsdp'=8] {'fsdp'}, dimensions={0}, use_global_device_ids=true | all-gather | bytes 34560 | tf_op jit(solution)/shard_map/all_gather | solution.py:93
  54.6 141.9 %all-gather.6.cloned.1.call-done = bf16[1280,5120]{1,0:T(8,128)(2,1)} async-done(((bf16[160,5120]{1,0:T(8,128)(2,1)}), bf16[1280,5120]{1,0:T(8,128)(2,1)}) %all-gather.6.cloned.1.call-update) | async-done | bytes 13107216 | tf_op jit(solution)/shard_map/all_gather | solution.py:91
  196.5 5.3 fusion.22
  203.5 3.7 fusion.122
  207.5 489.4 %all-gather.8.cloned.1.call-done = bf16[1280,10240]{1,0:T(8,128)(2,1)} async-done(((bf16[160,10240]{1,0:T(8,128)(2,1)}), bf16[1280,10240]{1,0:T(8,128)(2,1)}) %all-gather.8.cloned.1.call-update) | async-done | bytes 26214416 | tf_op jit(solution)/shard_map/all_gather | solution.py:92
  696.8 5.9 fusion.16
  702.8 11.3 convert_reduce_fusion
  714.1 8.4 multiply_reduce_fusion.1
  723.0 3.3 fusion.57
  726.2 1.9 copy.148
  728.1 1.5 convolution_convert_fusion
  729.6 1.6 multiply_reduce_fusion
  732.3 1.0 fusion.107
  733.3 2.9 fusion.93
  736.2 9.2 pad_maximum_fusion.1
  745.6 13.1 fusion.115
  758.6 12.3 fusion.110
  770.9 34.1 %pad_maximum_fusion = f32[1280,10240]{1,0:T(8,128)} fusion(f32[1280,5120]{1,0:T(8,128)} %fusion.110, f32[1280,5120]{1,0:T(8,128)} %fusion.115), kind=kLoop, calls=%fused_computation | loop fusion | flops 13107200 | bytes 104857600 | tf_op jit(solution)/shard_map/concatenate | solution.py:212
  805.1 358.9 %reduce-scatter.7.cloned.1.call-done = f32[160,5120]{1,0:T(8,128)} async-done(((f32[1280,5120]{1,0:T(8,128)}), f32[160,5120]{1,0:T(8,128)}) %reduce-scatter.7.cloned.1.call-update) | async-done | bytes 3276816 | tf_op jit(solution)/shard_map/reduce_scatter | solution.py:203
  1164.0 9.6 fusion.29
  1173.7 811.0 %reduce-scatter.9.cloned.1.call-done = f32[160,10240]{1,0:T(8,128)} async-done(((f32[1280,10240]{1,0:T(8,128)}), f32[160,10240]{1,0:T(8,128)}) %reduce-scatter.9.cloned.1.call-update) | async-done | bytes 6553616 | tf_op jit(solution)/shard_map/reduce_scatter | solution.py:211
  1984.6 18.2 fusion.15
  2003.2 6.5 fusion.117
  2009.7 6.0 fusion.87
  2016.3 1.1 copy.153
  2017.6 1.7 fusion.90
  2019.3 1.7 pad_maximum_fusion.3
  2021.1 12.6 fusion.116
  2033.6 22.6 reduce-scatter.15.cloned.1.call-done
  2056.3 2.8 fusion.66
  2059.1 2.5 pad_maximum_fusion.2
  2065.3 1.1 fusion.86
  2066.4 13.2 fusion.54
  2079.6 42.7 %reduce-scatter.11.cloned.1.call-done = f32[12,160]{0,1:T(8,128)} async-done(((f32[12,1280]{0,1:T(8,128)}), f32[12,160]{0,1:T(8,128)}) %reduce-scatter.11.cloned.1.call-update) | async-done | bytes 7696 | tf_op jit(solution)/shard_map/reduce_scatter | solution.py:220
  2122.3 1.7 fusion.98
  2127.6 12.0 all-reduce
  2139.9 5.8 all_gather.26
  2146.3 8.3 maximum_bitcast_fusion.2
  2154.6 35.4 %all-gather.10.cloned.1.call-done = f32[3,160,5120]{2,1,0:T(8,128)} async-done(((f32[3,160,1280]{2,1,0:T(8,128)}), f32[3,160,5120]{2,1,0:T(8,128)}) %all-gather.10.cloned.1.call-update) | async-done | bytes 9830416 | tf_op jit(solution)/shard_map/all_gather | solution.py:272
  2190.0 3.3 fusion.61
  2193.4 19.0 maximum_bitcast_fusion
  2213.1 5.5 maximum_bitcast_fusion.1
  2218.6 97.3 %all-gather.12.cloned.1.call-done = f32[3,160,10240]{2,1,0:T(8,128)} async-done(((f32[3,160,2560]{2,1,0:T(8,128)}), f32[3,160,10240]{2,1,0:T(8,128)}) %all-gather.12.cloned.1.call-update) | async-done | bytes 19660816 | tf_op jit(solution)/shard_map/all_gather | solution.py:273
  2315.8 5.0 fusion.26
  2320.8 8.8 copy.180
  2329.6 15.0 copy.181
  (134 shorter events, 17.4 us)
Async XLA Ops:
  7.2 44.4 %copy-start = (s32[1,8]{1,0:T(1,128)S(1)}, s32[1,8]{1,0:T(1,128)}, u32[]{:S(2)}) copy-start(s32[1,8]{1,0:T(1,128)} %param.12) | copy-start | bytes 100
  7.2 189.3 %all-gather.6.cloned.1.call-start = ((), (), s32[]{:S(2)}) async-start(), calls=%async_computation.5 | async-start | bytes 14745600 | tf_op jit(solution)/shard_map/all_gather | solution.py:91
  10.6 686.3 %all-gather.8.cloned.1.call-start = ((), (), s32[]{:S(2)}) async-start(), calls=%async_computation.6 | async-start | bytes 29491200 | tf_op jit(solution)/shard_map/all_gather | solution.py:92
  15.6 0.7 copy-start.17
  15.6 38.6 %copy-start.5 = (bf16[128,1280]{1,0:T(8,128)(2,1)S(1)}, bf16[128,1280]{1,0:T(8,128)(2,1)}, u32[]{:S(2)}) copy-start(bf16[128,1280]{1,0:T(8,128)(2,1)} %param.10) | copy-start | bytes 983044
  15.6 1148.4 %reduce-scatter.7.cloned.1.call-start = ((), (), s32[]{:S(2)}) async-start(), calls=%async_computation.7 | async-start | bytes 29491200 | tf_op jit(solution)/shard_map/reduce_scatter | solution.py:203
  17.1 184.8 %copy-start.9 = (f32[1,12,160]{1,2,0:T(8,128)}, f32[1,12,160]{1,2,0:T(8,128)S(1)}, u32[]{:S(2)}) copy-start(f32[1,12,160]{1,2,0:T(8,128)S(1)} %copy.171) | copy-start | bytes 23044
  202.1 1.3 copy-start.11
  203.5 3.7 copy-start.12
  207.2 538.3 %copy-start.4 = (f32[128,1280]{1,0:T(8,128)}, f32[128,1280]{1,0:T(8,128)S(1)}, u32[]{:S(2)}) copy-start(f32[128,1280]{1,0:T(8,128)S(1)} %get-tuple-element.138) | copy-start | bytes 1966084
  696.8 5.9 copy-start.14
  702.8 11.3 copy-start.21
  714.1 8.4 copy-start.8
  729.6 3.7 copy-start.6
  731.2 1.1 copy-start.13
  745.5 13.2 copy-start.15
  745.5 1239.1 %reduce-scatter.9.cloned.1.call-start = ((), (), s32[]{:S(2)}) async-start(), calls=%async_computation.8 | async-start | bytes 58982400 | tf_op jit(solution)/shard_map/reduce_scatter | solution.py:211
  745.5 13.1 copy-start.22
  805.0 1212.5 %reduce-scatter.13.cloned.1.call-start = ((), (), s32[]{:S(2)}) async-start(), calls=%async_computation.10 | async-start | bytes 2048000 | tf_op jit(solution)/shard_map/reduce_scatter | solution.py:231
  1173.6 882.6 %reduce-scatter.15.cloned.1.call-start = ((), (), s32[]{:S(2)}) async-start(), calls=%async_computation.12 | async-start | bytes 4096000 | tf_op jit(solution)/shard_map/reduce_scatter | solution.py:237
  2002.9 119.4 %reduce-scatter.11.cloned.1.call-start = ((), (), s32[]{:S(2)}) async-start(), calls=%async_computation.9 | async-start | bytes 737280 | tf_op jit(solution)/shard_map/reduce_scatter | solution.py:220
  2003.2 6.5 copy-start.7
  2017.5 172.6 %all-gather.10.cloned.1.call-start = ((), (), s32[]{:S(2)}) async-start(), calls=%async_computation.11 | async-start | bytes 12288000 | tf_op jit(solution)/shard_map/all_gather | solution.py:272
  2021.0 294.8 %all-gather.12.cloned.1.call-start = ((), (), s32[]{:S(2)}) async-start(), calls=%async_computation.13 | async-start | bytes 24576000 | tf_op jit(solution)/shard_map/all_gather | solution.py:273
  2061.6 0.7 copy-start.18
  2061.6 2.4 copy-start.20
  2061.6 4.8 copy-start.19
  2066.4 55.9 %copy-start.10 = (f32[1,12,160]{1,2,0:T(8,128)S(1)}, f32[1,12,160]{1,2,0:T(8,128)}, u32[]{:S(2)}) copy-start(f32[1,12,160]{1,2,0:T(8,128)} %copy-done.9) | copy-start | bytes 23044
  2066.4 79.9 %copy-start.2 = (f32[160,5120]{1,0:T(8,128)S(1)}, f32[160,5120]{1,0:T(8,128)}, u32[]{:S(2)}) copy-start(f32[160,5120]{1,0:T(8,128)} %reduce-scatter.7.cloned.1.call-done) | copy-start | bytes 9830404
  2145.7 9.0 copy-start.16
  2193.3 19.0 slice-start
  2193.3 19.0 slice-start.1
  2193.3 19.7 copy-start.3
  2329.6 15.0 copy-start.1
Sparse Core Ops, SparseCore 0:
  10.8 185.6 all-gather.5
  198.6 498.2 all-gather.7
  745.6 418.3 reduce-scatter.6
  1167.8 816.8 reduce-scatter.8
  1987.6 27.6 reduce-scatter.12
  2017.7 38.5 reduce-scatter.14
  2059.5 62.7 reduce-scatter.10
  2123.9 66.1 all-gather.9
  2191.6 124.1 all-gather.11
where the time goes:
time: 2360 us; the launch traced here: 2350 us
  waiting for transfers between devices  2000 us (85%)
  other arithmetic  119 us (5%)
  matrix products  91.1 us (4%)
  local copies, waits for them, and re-layouts  74.3 us (3%)
  blocking collectives  51.4 us (2%)
    reduce_scatter x1, waiting for transfers between devices, shards(): lax.psum_scatter(jnp.concatenate([contract_rows(layer_two, grad_pre), con...  811 us
    all_gather x1, waiting for transfers between devices, shards(): lax.all_gather(copies[1], 'fsdp', axis=0, tiled=True)  489 us
    reduce_scatter x1, waiting for transfers between devices, shards(): lax.psum_scatter(jnp.concatenate([contract_rows(layer_one, grad_qkv), con...  359 us
    all_gather x1, waiting for transfers between devices, shards(): lax.all_gather(copies[0], 'fsdp', axis=0, tiled=True)  142 us
    all_gather x1, waiting for transfers between devices, shards(): lax.all_gather(part_feedforward, 'rep', axis=2, tiled=True)  97.3 us
  transfers between devices with their start and end apart: 9, of which 8 were waited for; matrix products, arithmetic and copies ran while one was open for 9% of the time, Pallas kernels for 0%

commit v1 on v0

--- a/solution.py
+++ b/solution.py
@@ -3,6 +3,7 @@
 import jax.numpy as jnp
 from jax import lax
 from jax.sharding import PartitionSpec as P
+from jax.lax import axis_index, axis_size, ppermute
 
 D = 1280
 HEADS = 16
@@ -87,8 +88,21 @@
         masters[1].astype(jnp.bfloat16),
         masters[2].astype(jnp.bfloat16),
     )
+
+    def review_pages(incoming_x, group_axis):
+        d_next = axis_index(group_axis)
+        v_now = axis_size(group_axis)
+        piece_now, side_arr, found_now = (v_now, d_next, incoming_x.shape[0])
+        newest, field_out = (incoming_x, 1)
+        while field_out < piece_now:
+            u1 = tuple(((q, (q - field_out) % piece_now) for q in range(piece_now)))
+            seen_now = ppermute(newest, axis_name=group_axis, perm=u1)
+            newest = jnp.concatenate([newest, seen_now], 0)
+            field_out = 2 * field_out
+        return jnp.roll(newest, side_arr * found_now, 0)
+
     full_attention, full_feedforward, full_vectors = (
-        lax.all_gather(copies[0], "fsdp", axis=0, tiled=True),
+        review_pages(copies[0], "fsdp"),
         lax.all_gather(copies[1], "fsdp", axis=0, tiled=True),
         lax.all_gather(copies[2], "fsdp", axis=1, tiled=True),
     )

time: 2360 us -> 2500 us (1.059)
  blocking collectives: 51.4 us -> 457 us
  waiting for transfers between devices: 2000 us -> 1690 us
  local copies, waits for them, and re-layouts: 74.3 us -> 99.7 us
    all_gather x1, waiting for transfers between devices: 489 us -> 0.02 us  [shards(): lax.all_gather(copies[1], 'fsdp', axis=0, tiled=True)]
    all_gather x1, blocking collectives: 33.6 us -> 440 us  [shards(): lax.all_gather(copies[2], 'fsdp', axis=1, tiled=True)]
    ppermute x0 -> x3, waiting for transfers between devices: none -> 233 us  [review_pages(): seen_now = ppermute(newest, axis_name=group_axis, perm=u1)]
    all_gather x1, waiting for transfers between devices: 142 us -> 89.5 us  [shards(): lax.all_gather(copies[0], 'fsdp', axis=0, tiled=True)]
  transfers between devices with their start and end apart: 9 -> 12, of which waited for: 8 -> 9; matrix products, arithmetic and copies ran while one was open for 9% -> 11% of each run, Pallas kernels for 0% -> 0%
where the time goes in v1:
time: 2500 us
  waiting for transfers between devices  1690 us (68%)
  blocking collectives  457 us (18%)
  other arithmetic  129 us (5%)
  local copies, waits for them, and re-layouts  99.7 us (4%)
  matrix products  93.4 us (4%)
    reduce_scatter x1, waiting for transfers between devices, shards(): lax.psum_scatter(jnp.concatenate([contract_rows(layer_two, grad_pre), con...  810 us
    all_gather x1, blocking collectives, shards(): lax.all_gather(copies[2], 'fsdp', axis=1, tiled=True)  440 us
    reduce_scatter x1, waiting for transfers between devices, shards(): lax.psum_scatter(jnp.concatenate([contract_rows(layer_one, grad_qkv), con...  356 us
    ppermute x3, waiting for transfers between devices, review_pages(): seen_now = ppermute(newest, axis_name=group_axis, perm=u1)  233 us
    all_gather x1, waiting for transfers between devices, shards(): lax.all_gather(part_feedforward, 'rep', axis=2, tiled=True)  97.3 us
    all_gather x1, waiting for transfers between devices, shards(): lax.all_gather(copies[0], 'fsdp', axis=0, tiled=True)  89.5 us
  transfers between devices with their start and end apart: 12, of which 9 were waited for; matrix products, arithmetic and copies ran while one was open for 11% of the time, Pallas kernels for 0%

profile of v1, /device:TPU:0, one launch (start us, length us, event | category | flops | bytes accessed | tf_op | source)
XLA Modules:
  0.0 2496.0 jit_solution(14411182239107334273)
XLA Ops:
  7.2 5.0 bitcast_convert_fusion
  12.3 4.1 constant_dynamic-update-slice_fusion.7
  16.4 6.0 collective-permute-start
  22.5 101.1 %collective-permute-done = bf16[160,5120]{1,0:T(8,128)(2,1)S(1)} collective-permute-done((bf16[160,5120]{1,0:T(8,128)(2,1)}, bf16[160,5120]{1,0:T(8,128)(2,1)S(1)}, u32[]{:S(2)}, u32[]{:S(2)}) %collective-permute-start) | collective-permute-done | bytes 1638432 | tf_op jit(solution)/shard_map/ppermute | solution.py:99
  126.6 4.7 collective-permute-start.1
  131.3 131.8 %collective-permute-done.1 = bf16[320,5120]{1,0:T(8,128)(2,1)S(1)} collective-permute-done((bf16[320,5120]{1,0:T(8,128)(2,1)S(1)}, bf16[320,5120]{1,0:T(8,128)(2,1)S(1)}, u32[]{:S(2)}, u32[]{:S(2)}) %collective-permute-start.1) | collective-permute-done | bytes 3276832 | tf_op jit(solution)/shard_map/ppermute | solution.py:99
  263.1 5.1 pad_maximum_fusion.2
  268.2 2.7 collective-permute-start.2
  271.8 439.8 %all-gather = bf16[8,160,12]{1,2,0:T(8,128)(2,1)S(1)} all-gather(bf16[1,160,12]{1,2,0:T(8,128)(2,1)S(1)} %copy.142), channel_id=1, replica_groups=mesh['rep'=4,'fsdp'=8] {'fsdp'}, dimensions={0}, use_global_device_ids=true | all-gather | bytes 34560 | tf_op jit(solution)/shard_map/all_gather | solution.py:107
  718.6 2.7 constant_dynamic-update-slice_fusion.6
  723.3 6.0 constant_dynamic-update-slice_fusion.4
  729.3 2.8 constant_dynamic-update-slice_fusion.3
  735.3 6.1 constant_dynamic-update-slice_fusion
  741.4 7.1 fusion.22
  750.1 4.2 fusion.123
  754.7 6.4 fusion.16
  761.1 11.4 convert_reduce_fusion
  772.5 7.9 multiply_reduce_fusion.1
  780.9 89.5 %all-gather.8.cloned.1.call-done = bf16[1280,5120]{1,0:T(8,128)(2,1)} async-done(((bf16[160,5120]{1,0:T(8,128)(2,1)}), bf16[1280,5120]{1,0:T(8,128)(2,1)}) %all-gather.8.cloned.1.call-update) | async-done | bytes 13107216 | tf_op jit(solution)/shard_map/all_gather | solution.py:154
  870.4 3.3 fusion.57
  880.7 2.9 fusion.93
  883.7 9.2 pad_maximum_fusion.1
  893.0 13.1 fusion.116
  906.1 12.3 fusion.111
  918.4 35.4 %pad_maximum_fusion = f32[1280,10240]{1,0:T(8,128)} fusion(f32[1280,5120]{1,0:T(8,128)} %fusion.111, f32[1280,5120]{1,0:T(8,128)} %fusion.116), kind=kLoop, calls=%fused_computation | loop fusion | flops 13107200 | bytes 104857600 | tf_op jit(solution)/shard_map/concatenate | solution.py:226
  953.8 355.7 %reduce-scatter.7.cloned.1.call-done = f32[160,5120]{1,0:T(8,128)} async-done(((f32[1280,5120]{1,0:T(8,128)}), f32[160,5120]{1,0:T(8,128)}) %reduce-scatter.7.cloned.1.call-update) | async-done | bytes 3276816 | tf_op jit(solution)/shard_map/reduce_scatter | solution.py:217
  1309.5 9.6 fusion.33
  1319.2 810.1 %reduce-scatter.9.cloned.1.call-done = f32[160,10240]{1,0:T(8,128)} async-done(((f32[1280,10240]{1,0:T(8,128)}), f32[160,10240]{1,0:T(8,128)}) %reduce-scatter.9.cloned.1.call-update) | async-done | bytes 6553616 | tf_op jit(solution)/shard_map/reduce_scatter | solution.py:225
  2129.3 18.2 fusion.15
  2148.0 6.5 fusion.118
  2154.5 6.0 fusion.87
  2165.9 12.6 fusion.117
  2178.5 22.4 reduce-scatter.15.cloned.1.call-done
  2200.9 2.8 fusion.66
  2203.7 2.5 pad_maximum_fusion.3
  2211.0 13.2 fusion.54
  2224.2 42.8 %reduce-scatter.11.cloned.1.call-done = f32[12,160]{0,1:T(8,128)} async-done(((f32[12,1280]{0,1:T(8,128)}), f32[12,160]{0,1:T(8,128)}) %reduce-scatter.11.cloned.1.call-update) | async-done | bytes 7696 | tf_op jit(solution)/shard_map/reduce_scatter | solution.py:234
  2272.2 12.0 all-reduce
  2284.6 5.7 all_gather.25
  2290.9 8.3 maximum_bitcast_fusion.2
  2299.2 35.5 %all-gather.10.cloned.1.call-done = f32[3,160,5120]{2,1,0:T(8,128)} async-done(((f32[3,160,1280]{2,1,0:T(8,128)}), f32[3,160,5120]{2,1,0:T(8,128)}) %all-gather.10.cloned.1.call-update) | async-done | bytes 9830416 | tf_op jit(solution)/shard_map/all_gather | solution.py:286
  2334.7 3.3 fusion.61
  2338.0 19.0 maximum_bitcast_fusion
  2357.7 5.5 maximum_bitcast_fusion.1
  2363.2 97.3 %all-gather.12.cloned.1.call-done = f32[3,160,10240]{2,1,0:T(8,128)} async-done(((f32[3,160,2560]{2,1,0:T(8,128)}), f32[3,160,10240]{2,1,0:T(8,128)}) %all-gather.12.cloned.1.call-update) | async-done | bytes 19660816 | tf_op jit(solution)/shard_map/all_gather | solution.py:287
  2460.5 5.0 fusion.26
  2465.4 8.8 copy.187
  2474.2 15.0 copy.188
  (155 shorter events, 41.6 us)
Async XLA Ops:
  7.2 705.3 %copy-start = (s32[1,8]{1,0:T(1,128)S(1)}, s32[1,8]{1,0:T(1,128)}, u32[]{:S(2)}) copy-start(s32[1,8]{1,0:T(1,128)} %param.12) | copy-start | bytes 100
  7.2 747.5 %all-gather.6.cloned.1.call-start = ((), (), s32[]{:S(2)}) async-start(), calls=%async_computation.5 | async-start | bytes 29491200 | tf_op jit(solution)/shard_map/all_gather | solution.py:106
  12.2 858.2 %all-gather.8.cloned.1.call-start = ((), (), s32[]{:S(2)}) async-start(), calls=%async_computation.6 | async-start | bytes 14745600 | tf_op jit(solution)/shard_map/all_gather | solution.py:154
  16.4 107.2 %collective-permute-start = (bf16[160,5120]{1,0:T(8,128)(2,1)}, bf16[160,5120]{1,0:T(8,128)(2,1)S(1)}, u32[]{:S(2)}, u32[]{:S(2)}) collective-permute-start(bf16[160,5120]{1,0:T(8,128)(2,1)} %get-tuple-element.109), channel_id=1, source_target_pairs={{0,7},{1,0},{2,1},{3,2},{4,3},{5,4},{6,5},{7,6},{8,15},{9,8},{10,9... | collective-permute-start | bytes 4915208 | tf_op jit(solution)/shard_map/ppermute | solution.py:99
  22.4 1287.0 %reduce-scatter.7.cloned.1.call-start = ((), (), s32[]{:S(2)}) async-start(), calls=%async_computation.7 | async-start | bytes 29491200 | tf_op jit(solution)/shard_map/reduce_scatter | solution.py:217
  123.6 1.2 copy-start.2
  126.6 144.4 %copy-start.20 = (f32[2,12,160]{2,0,1:T(2,128)S(1)}, f32[2,12,160]{2,0,1:T(2,128)}, u32[]{:S(2)}) copy-start(f32[2,12,160]{2,0,1:T(2,128)} %param.16) | copy-start | bytes 46084
  126.6 136.5 %collective-permute-start.1 = (bf16[320,5120]{1,0:T(8,128)(2,1)S(1)}, bf16[320,5120]{1,0:T(8,128)(2,1)S(1)}, u32[]{:S(2)}, u32[]{:S(2)}) collective-permute-start(bf16[320,5120]{1,0:T(8,128)(2,1)S(1)} %pad_maximum_fusion.4), channel_id=1, source_target_pairs={{0,6},{1,7},{2,0},{3,1},{4,2},{5,3},{6,4},{7,5},{8,14},{9,15},{10,... | collective-permute-start | bytes 9830408 | tf_op jit(solution)/shard_map/ppermute | solution.py:99
  268.2 455.0 %collective-permute-start.2 = (bf16[640,5120]{1,0:T(8,128)(2,1)}, bf16[640,5120]{1,0:T(8,128)(2,1)}, u32[]{:S(2)}, u32[]{:S(2)}) collective-permute-start(bf16[640,5120]{1,0:T(8,128)(2,1)} %pad_maximum_fusion.2), channel_id=1, source_target_pairs={{0,4},{1,5},{2,6},{3,7},{4,0},{5,1},{6,2},{7,3},{8,12},{9,13},{10,... | collective-permute-start | bytes 19660808 | tf_op jit(solution)/shard_map/ppermute | solution.py:99
  271.7 451.6 %copy-start.13 = (f32[1,12,160]{1,2,0:T(8,128)}, f32[1,12,160]{1,2,0:T(8,128)S(1)}, u32[]{:S(2)}) copy-start(f32[1,12,160]{1,2,0:T(8,128)S(1)} %copy.171) | copy-start | bytes 23044
  711.7 2.0 copy-start.18
  729.3 2.8 copy-start.3
  735.3 6.1 copy-start.6
  748.8 1.3 copy-start.15
  750.1 4.5 copy-start.11
  754.4 138.6 %copy-start.7 = (f32[128,1280]{1,0:T(8,128)}, f32[128,1280]{1,0:T(8,128)S(1)}, u32[]{:S(2)}) copy-start(f32[128,1280]{1,0:T(8,128)S(1)} %get-tuple-element.140) | copy-start | bytes 1966084
  754.7 6.4 copy-start.16
  761.1 11.4 copy-start.24
  772.5 7.9 copy-start.10
  877.0 3.7 copy-start.8
  878.6 1.1 copy-start.12
  892.9 13.2 copy-start.17
  892.9 1236.3 %reduce-scatter.9.cloned.1.call-start = ((), (), s32[]{:S(2)}) async-start(), calls=%async_computation.8 | async-start | bytes 58982400 | tf_op jit(solution)/shard_map/reduce_scatter | solution.py:225
  893.0 13.1 copy-start.25
  953.8 1208.6 %reduce-scatter.13.cloned.1.call-start = ((), (), s32[]{:S(2)}) async-start(), calls=%async_computation.10 | async-start | bytes 2048000 | tf_op jit(solution)/shard_map/reduce_scatter | solution.py:245
  1319.1 881.8 %reduce-scatter.15.cloned.1.call-start = ((), (), s32[]{:S(2)}) async-start(), calls=%async_computation.12 | async-start | bytes 4096000 | tf_op jit(solution)/shard_map/reduce_scatter | solution.py:251
  2147.5 119.4 %reduce-scatter.11.cloned.1.call-start = ((), (), s32[]{:S(2)}) async-start(), calls=%async_computation.9 | async-start | bytes 737280 | tf_op jit(solution)/shard_map/reduce_scatter | solution.py:234
  2148.0 6.5 copy-start.9
  2162.3 172.4 %all-gather.10.cloned.1.call-start = ((), (), s32[]{:S(2)}) async-start(), calls=%async_computation.11 | async-start | bytes 12288000 | tf_op jit(solution)/shard_map/all_gather | solution.py:286
  2165.8 294.7 %all-gather.12.cloned.1.call-start = ((), (), s32[]{:S(2)}) async-start(), calls=%async_computation.13 | async-start | bytes 24576000 | tf_op jit(solution)/shard_map/all_gather | solution.py:287
  2206.2 0.7 copy-start.21
  2206.2 2.4 copy-start.23
  2206.2 4.8 copy-start.22
  2211.0 55.9 %copy-start.14 = (f32[1,12,160]{1,2,0:T(8,128)S(1)}, f32[1,12,160]{1,2,0:T(8,128)}, u32[]{:S(2)}) copy-start(f32[1,12,160]{1,2,0:T(8,128)} %copy-done.13) | copy-start | bytes 23044
  2211.0 79.8 %copy-start.4 = (f32[160,5120]{1,0:T(8,128)S(1)}, f32[160,5120]{1,0:T(8,128)}, u32[]{:S(2)}) copy-start(f32[160,5120]{1,0:T(8,128)} %reduce-scatter.7.cloned.1.call-done) | copy-start | bytes 9830404
  2290.3 9.0 copy-start.19
  2338.0 19.0 slice-start
  2338.0 19.0 slice-start.1
  2338.0 19.7 copy-start.5
  2474.2 15.0 copy-start.1
Sparse Core Ops, SparseCore 0:
  12.4 540.4 all-gather.5
  555.6 314.7 all-gather.7
  893.0 416.4 reduce-scatter.6
  1313.2 815.9 reduce-scatter.8
  2132.2 27.5 reduce-scatter.12
  2162.3 38.5 reduce-scatter.14
  2204.2 62.7 reduce-scatter.10
  2268.5 66.1 all-gather.9
  2336.3 124.1 all-gather.11
